TPU v7x, 32 devices: a whole 2x2x4 slice. The times are simulated.
32 devices in a mesh: expert: 16 (over z, y, x), tensor: 2 (over core).
Axes of the slice: x: 2, y: 2, z: 4, core: 2. Of those that a mesh axis runs over, the one named last changes fastest.
Arguments:
- states: bfloat16 [2048, 1536], P('expert'), may hold values from -60 to 60
- norm_gain: float32 [1536], replicated, may hold values from 0.25 to 1.75
- router: bfloat16 [1536, 8], replicated, may hold values from -0.15625 to 0.15625
- w_gate: bfloat16 [16, 1536, 2048], P('expert', None, 'tensor'), may hold values from -0.15625 to 0.15625
- w_up: bfloat16 [16, 1536, 2048], P('expert', None, 'tensor'), may hold values from -0.15625 to 0.15625
- w_down: bfloat16 [16, 2048, 1536], P('expert', 'tensor'), may hold values from -0.09375 to 0.09375
- expert_ids: int32 [2048, 2], P('expert'), may hold values from 0 to 7, as said below
- slot_pos: int32 [2048, 2], P('expert'), may hold values from 0 to 41, as said below
- keep_mask: int32 [2048, 2], P('expert'), may hold values from 0 to 1, as said below
Outputs:
- next_states: bfloat16 [2048, 1536], P('expert')
Inputs may be any that keep to these rules, and one draw needn't show every extreme that they name: `expert_ids`: each row names two different experts; in every block of 128 rows one expert is named by more than 41 rows. `slot_pos`: for each choice, the number of earlier choices of the same expert within the same block of 128 rows, counted row by row with a row's first choice before its second, or 41 where that number is 41 or more. `keep_mask`: 1 exactly where slot_pos is under 41; in every block of 128 rows some expert has all 41 slots filled.
All inputs are finite; a program needn't handle non-finite values.
Results may differ from a plain program's by a relative error of at most 0.0038.
Values may be sent and summed in bfloat16 or wider, within the bound.
A program may use at most 64 MiB of HBM per device.

v0:
```python
import jax
import jax.numpy as jnp
from jax import lax
from jax.sharding import PartitionSpec as P


def per_device(states, norm_gain, router, w_gate, w_up, w_down, expert_ids, slot_pos, keep_mask):
    tok_rows, feat_width = states.shape
    groups = lax.axis_size("expert")
    all_experts = router.shape[1]
    holders = groups // all_experts
    capacity = max(2, 5 * tok_rows // (2 * all_experts) + 1)
    tensor_count = lax.axis_size("tensor")
    share_width = feat_width // tensor_count
    tensor_rank = lax.axis_index("tensor")
    values = states.astype(jnp.float32)
    normed = (
        values * lax.rsqrt(jnp.mean(values * values, axis=-1, keepdims=True) + 1e-06) * norm_gain
    ).astype(jnp.bfloat16)
    logits = jnp.dot(normed, router, preferred_element_type=jnp.float32)
    columns = lax.broadcasted_iota(jnp.int32, (tok_rows, all_experts), 1)
    chosen = jnp.stack(
        [
            jnp.sum(jnp.where(columns == expert_ids[:, pick][:, None], logits, 0.0), axis=1)
            for pick in range(expert_ids.shape[1])
        ],
        axis=1,
    )
    gate_score = jax.nn.sigmoid(chosen)
    weight = gate_score / jnp.sum(gate_score, axis=1, keepdims=True)
    is_kept = keep_mask > 0
    slot_index = jnp.where(is_kept, expert_ids * capacity + slot_pos, -1)
    targets = lax.broadcasted_iota(jnp.int32, (all_experts * capacity, tok_rows), 0)
    dispatch_table = jnp.any(targets[:, :, None] == slot_index[None, :, :], axis=-1).astype(
        jnp.bfloat16
    )
    outgoing = jnp.dot(dispatch_table, normed, preferred_element_type=jnp.float32).astype(
        jnp.bfloat16
    )
    outgoing = jnp.repeat(outgoing.reshape(all_experts, capacity, feat_width), holders, axis=0)
    arrived = lax.all_to_all(outgoing, "expert", split_axis=0, concat_axis=0, tiled=True)
    flat_rows = arrived.reshape(groups * capacity, feat_width)
    gate_act = jnp.dot(flat_rows, w_gate[0], preferred_element_type=jnp.float32)
    up_act = jnp.dot(flat_rows, w_up[0], preferred_element_type=jnp.float32)
    hidden = (jax.nn.silu(gate_act) * up_act).astype(jnp.bfloat16)
    partial_out = jnp.dot(hidden, w_down[0], preferred_element_type=jnp.float32)
    partial_out = partial_out.reshape(groups, capacity, feat_width)
    summed = lax.psum_scatter(
        partial_out.astype(jnp.bfloat16), "tensor", scatter_dimension=2, tiled=True
    ).astype(jnp.float32)
    returned = lax.all_to_all(
        summed.astype(jnp.bfloat16), "expert", split_axis=0, concat_axis=0, tiled=True
    ).astype(summed.dtype)
    residual = lax.dynamic_slice_in_dim(values, tensor_rank * share_width, share_width, 1)
    out_width = returned.shape[2]
    expert_out = jnp.sum(
        returned.reshape(all_experts, holders, capacity, out_width), axis=1
    ).astype(jnp.bfloat16)
    flat_out = expert_out.reshape(all_experts * capacity, out_width)
    picked = jnp.take(flat_out, jnp.maximum(slot_index, 0), axis=0).astype(jnp.float32)
    factor = jnp.where(is_kept, weight, 0.0)
    combined = jnp.sum(factor[:, :, None] * picked, axis=1)
    next_states = (residual + combined).astype(jnp.bfloat16)
    next_states = lax.all_gather(next_states, "tensor", axis=1, tiled=True)
    return next_states


def solution(mesh):
    placed = (
        P("expert", None),
        P(),
        P(),
        P("expert", None, "tensor"),
        P("expert", None, "tensor"),
        P("expert", "tensor", None),
        P("expert", None),
        P("expert", None),
        P("expert", None),
    )
    return jax.shard_map(
        per_device, mesh=mesh, in_specs=placed, out_specs=P("expert", None), check_vma=False
    )
```

profile of v0, /device:TPU:0, one launch (start us, length us, event | category | flops | bytes accessed | tf_op | source)
XLA Modules:
  0.0 162.3 jit_solution(2952750581993070489)
XLA Ops:
  6.5 1.4 broadcast_compare_fusion
  8.0 1.2 multiply_reduce_fusion.1
  9.7 2.5 %convolution_convert_fusion.1 = bf16[328,1536]{1,0:T(8,128)(2,1)} fusion(pred[328,128]{1,0:T(8,128)(4,1)S(1)} %fusion.7, f32[1536]{0:T(1024)} %param.10, f32[128]{0:T(128)S(1)} %add_rsqrt_fusion, bf16[128,1536]{1,0:T(8,128)(2,1)} %param.9), kind=kOutput, calls=%fused_computation.7 | convolution fusion | flops 130265088 | bytes 1449472 | tf_op jit(solution)/shard_map/dot_general | solution.py:37
  12.2 2.5 %reshape.37 = bf16[8,41,1536]{2,1,0:T(8,128)(2,1)} reshape(bf16[328,1536]{1,0:T(8,128)(2,1)} %convolution_convert_fusion.1) | data formatting | bytes 2015232 | tf_op jit(solution)/shard_map/reshape | solution.py:40
  14.8 1.5 broadcast_in_dim.38
  16.3 63.2 %all_to_all.10 = bf16[16,41,1536]{2,1,0:T(8,128)(2,1)} all-to-all(bf16[16,41,1536]{2,1,0:T(8,128)(2,1)S(1)} %bitcast.26), channel_id=1, replica_groups=mesh['expert'=16,'tensor'=2] {'expert'}, dimensions={0} | all-to-all | bytes 4030464 | tf_op jit(solution)/shard_map/all_to_all | solution.py:41
  79.5 2.9 %reshape.39 = bf16[656,1536]{1,0:T(8,128)(2,1)} reshape(bf16[16,41,1536]{2,1,0:T(8,128)(2,1)} %all_to_all.10) | data formatting | bytes 4030464 | tf_op jit(solution)/shard_map/reshape | solution.py:42
  82.4 4.9 %fusion.3 = f32[656,1024]{1,0:T(8,128)S(1)} fusion(bf16[656,1536]{1,0:T(8,128)(2,1)} %reshape.39, bf16[1,1536,1024]{2,1,0:T(8,128)(2,1)} %param.12), kind=kOutput, calls=%fused_computation.5 | convolution fusion | flops 2063597568 | bytes 7847936 | tf_op jit(solution)/shard_map/dot_general | solution.py:43
  87.4 3.5 %multiply_convert_fusion = bf16[656,1024]{1,0:T(8,128)(2,1)} fusion(f32[656,1024]{1,0:T(8,128)S(1)} %fusion.3, bf16[656,1536]{1,0:T(8,128)(2,1)S(1)} %copy-done.2, bf16[1,1536,1024]{2,1,0:T(8,128)(2,1)S(1)} %copy-done.4), kind=kOutput, calls=%fused_computation.8 | convolution fusion | flops 2067628032 | bytes 9191424 | tf_op jit(solution)/shard_map/dot_general | solution.py:44
  90.9 2.5 %dot_general.21 = bf16[16,41,1024]{2,1,0:T(8,128)(2,1)} reshape(bf16[656,1024]{1,0:T(8,128)(2,1)} %multiply_convert_fusion) | data formatting | bytes 2686976 | tf_op jit(solution)/shard_map/dot_general | solution.py:46
  93.3 5.3 %convolution_convert_fusion = bf16[16,41,1536]{2,1,0:T(8,128)(2,1)} fusion(bf16[16,41,1024]{2,1,0:T(8,128)(2,1)} %dot_general.21, bf16[1,1024,1536]{2,1,0:T(8,128)(2,1)S(1)} %copy-done), kind=kOutput, calls=%fused_computation.1 | convolution fusion | flops 2064605184 | bytes 6504448 | tf_op jit(solution)/shard_map/dot_general | solution.py:46
  98.6 7.9 %reduce-scatter.2.cloned.1.call-done = bf16[16,41,768]{2,1,0:T(8,128)(2,1)} async-done(((bf16[16,41,1536]{2,1,0:T(8,128)(2,1)}), bf16[16,41,768]{2,1,0:T(8,128)(2,1)}) %reduce-scatter.2.cloned.1.call-update) | async-done | bytes 1007632 | tf_op jit(solution)/shard_map/reduce_scatter | solution.py:48
  106.5 6.9 %all-to-all-start.1 = ((bf16[16,41,768]{2,1,0:T(8,128)(2,1)}), bf16[16,41,768]{2,1,0:T(8,128)(2,1)}, u32[]{:S(2)}, u32[]{:S(2)}) async-start(bf16[16,41,768]{2,1,0:T(8,128)(2,1)} %reduce-scatter.2.cloned.1.call-done), calls=%async_computation.2 | async-start | bytes 2359296 | tf_op jit(solution)/shard_map/all_to_all | solution.py:51
  113.5 1.0 convert_element_type.32
  115.2 1.6 reshape.44
  118.3 1.0 select_reduce_fusion.1
  121.5 19.1 %all-to-all-done.1 = bf16[16,41,768]{2,1,0:T(8,128)(2,1)} async-done(((bf16[16,41,768]{2,1,0:T(8,128)(2,1)}), bf16[16,41,768]{2,1,0:T(8,128)(2,1)}, u32[]{:S(2)}, u32[]{:S(2)}) %all-to-all-start.1) | async-done | bytes 1007648 | tf_op jit(solution)/shard_map/all_to_all | solution.py:51
  140.6 2.5 %bitcast_reduce_fusion = bf16[8,41,768]{2,1,0:T(8,128)(2,1)} fusion(bf16[16,41,768]{2,1,0:T(8,128)(2,1)} %all-to-all-done.1), kind=kLoop, calls=%fused_computation.9 | loop fusion | flops 251904 | bytes 1511424 | tf_op jit(solution)/shard_map/reduce_sum | solution.py:56
  143.0 2.0 %convert_element_type.38 = bf16[328,768]{1,0:T(8,128)(2,1)} reshape(bf16[8,41,768]{2,1,0:T(8,128)(2,1)} %bitcast_reduce_fusion) | data formatting | bytes 1007616 | tf_op jit(solution)/shard_map/convert_element_type | solution.py:58
  145.1 3.2 %gather_fusion = bf16[256,768]{1,0:T(8,128)(2,1)} fusion(bf16[328,768]{1,0:T(8,128)(2,1)} %convert_element_type.38, s32[1024]{0:T(1024)S(1)} %pad_clamp_fusion), kind=kCustom, calls=%fused_computation | custom fusion | bytes 787456 | tf_op jit(solution)/shard_map/jit(_take)/gather | solution.py:60
  148.3 1.1 reshape.43
  149.5 2.1 %multiply_reduce_fusion = f32[128,768]{1,0:T(8,128)S(1)} fusion(bf16[128,2,768]{2,1,0:T(2,128)(2,1)S(1)} %reshape.43, pred[128,2]{1,0:T(8,128)(4,1)S(1)} %copy.18, f32[128,2]{1,0:T(8,128)} %copy.17), kind=kLoop, calls=%fused_computation.10 | loop fusion | flops 688128 | bytes 787712 | tf_op jit(solution)/shard_map/reduce_sum | solution.py:62
  151.6 1.1 add_convert_fusion
  152.6 2.1 %all_gather.3 = bf16[128,1536]{1,0:T(8,128)(2,1)S(1)} all-gather(bf16[128,768]{1,0:T(8,128)(2,1)S(1)} %add_convert_fusion), channel_id=1, replica_groups=mesh['expert'=16,'tensor'=2] {'tensor'}, dimensions={1}, use_global_device_ids=true | all-gather | bytes 589824 | tf_op jit(solution)/shard_map/all_gather | solution.py:64
  (23 shorter events, 5.8 us)
Async XLA Ops:
  6.5 86.8 %copy-start = (bf16[1,1024,1536]{2,1,0:T(8,128)(2,1)S(1)}, bf16[1,1024,1536]{2,1,0:T(8,128)(2,1)}, u32[]{:S(2)}) copy-start(bf16[1,1024,1536]{2,1,0:T(8,128)(2,1)} %param.14) | copy-start | bytes 9437188
  6.5 100.0 %reduce-scatter.2.cloned.1.call-start = ((), (), s32[]{:S(2)}) async-start(), calls=%async_computation.3 | async-start | bytes 3538944 | tf_op jit(solution)/shard_map/reduce_scatter | solution.py:48
  9.2 0.5 copy-start.3
  82.4 4.9 %copy-start.2 = (bf16[656,1536]{1,0:T(8,128)(2,1)S(1)}, bf16[656,1536]{1,0:T(8,128)(2,1)}, u32[]{:S(2)}) copy-start(bf16[656,1536]{1,0:T(8,128)(2,1)} %reshape.39) | copy-start | bytes 6045700
  82.4 4.9 %copy-start.4 = (bf16[1,1536,1024]{2,1,0:T(8,128)(2,1)S(1)}, bf16[1,1536,1024]{2,1,0:T(8,128)(2,1)}, u32[]{:S(2)}) copy-start(bf16[1,1536,1024]{2,1,0:T(8,128)(2,1)} %param.13) | copy-start | bytes 9437188
  98.6 14.8 %copy-start.1 = (bf16[128,1536]{1,0:T(8,128)(2,1)S(1)}, bf16[128,1536]{1,0:T(8,128)(2,1)}, u32[]{:S(2)}) copy-start(bf16[128,1536]{1,0:T(8,128)(2,1)} %param.9) | copy-start | bytes 1179652
  106.5 34.1 %all-to-all-start.1 = ((bf16[16,41,768]{2,1,0:T(8,128)(2,1)}), bf16[16,41,768]{2,1,0:T(8,128)(2,1)}, u32[]{:S(2)}, u32[]{:S(2)}) async-start(bf16[16,41,768]{2,1,0:T(8,128)(2,1)} %reduce-scatter.2.cloned.1.call-done), calls=%async_computation.2 | async-start | bytes 2359296 | tf_op jit(solution)/shard_map/all_to_all | solution.py:51
Sparse Core Ops, SparseCore 0:
  98.8 7.6 reduce-scatter.1
where the time goes:
time: 164 us; the launch traced here: 162 us
  blocking collectives  65.3 us (40%)
  waiting for transfers between devices  26.9 us (16%)
  local copies, waits for them, and re-layouts  21.7 us (13%)
  matrix products  17.2 us (10%)
  between operations  13.5 us (8%)
  other arithmetic  10.7 us (7%)
  starting transfers between devices  6.94 us (4%)
    all_to_all x1, blocking collectives, per_device(): lax.all_to_all(outgoing, 'expert', split_axis=0, concat_axis=0, tiled=True)  63.2 us
    all_to_all x1, waiting for transfers between devices, per_device(): lax.all_to_all(summed.astype(jnp.bfloat16), 'expert', split_axis=0, conca...  19.1 us
    reduce_scatter x1, waiting for transfers between devices, per_device(): lax.psum_scatter(partial_out.astype(jnp.bfloat16), 'tensor', scatter_dime...  7.85 us
    all_to_all x1, starting transfers between devices, per_device(): lax.all_to_all(summed.astype(jnp.bfloat16), 'expert', split_axis=0, conca...  6.94 us
    dot_general x1, matrix products, per_device(): partial_out = jnp.dot(hidden, w_down[0], preferred_element_type=jnp.float32)  5.27 us
    dot_general x1, matrix products, per_device(): gate_act = jnp.dot(flat_rows, w_gate[0], preferred_element_type=jnp.float32)  4.89 us
    gather x2, local copies, waits for them, and re-layouts, per_device(): jnp.take(flat_out, jnp.maximum(slot_index, 0), axis=0).astype(jnp.float32)  4.38 us
    dot_general x1, matrix products, per_device(): up_act = jnp.dot(flat_rows, w_up[0], preferred_element_type=jnp.float32)  3.51 us
  transfers between devices with their start and end apart: 2, of which 2 were waited for; matrix products, arithmetic and copies ran while one was open for 5% of the time, Pallas kernels for 0%

commit v1 on v0

v1 whole, which is shorter than its diff:
```python
import functools

import jax
import jax.numpy as jnp
from jax import lax
from jax.experimental import pallas as pl
from jax.experimental.pallas import tpu as pltpu
from jax.sharding import PartitionSpec as P

MESH = pl.DeviceIdType.MESH


def flip(value, mask):
    result = value
    bit = 1
    while bit <= mask:
        if mask & bit:
            result = result + bit * (1 - 2 * (value // bit % 2))
        bit *= 2
    return result


def peer_order(count):
    rest = list(range(1, count))
    return [0] + sorted(rest, key=lambda i: (bin(i).count("1"), -i))


def kernel(
    experts, capacity, padded,
    states_ref, gain_ref, router_ref, ids_ref, pos_ref, keep_ref, wg_hbm, wu_hbm, wd_hbm,
    out_ref,
    wg, wu, wd, sent, rows, hid, give, got, acc, cross, crossed, result, back, final,
    w_sem, a_send, a_recv, c_send, c_recv, x_send, x_recv,
    p_send, p_recv, r_send, r_recv, o_send, o_recv, f_send, f_recv,
):
    idx = lax.axis_index("expert")
    core = lax.axis_index("tensor")
    group, side = idx // 2, idx % 2
    other_side, other_core = 1 - side, 1 - core
    tok, width = states_ref.shape
    half = width // 2
    slots = experts * padded
    order = peer_order(experts)
    tile = 256
    neighbour = (group * 2 + other_side, core)
    sibling = (idx, other_core)

    loads = [
        pltpu.make_async_copy(src.at[0], dst, w_sem.at[n])
        for n, (src, dst) in enumerate(((wg_hbm, wg), (wu_hbm, wu), (wd_hbm, wd)))
    ]
    for load in loads:
        load.start()

    barrier = pltpu.get_barrier_semaphore()
    peers = [(flip(group, i) * 2 + side, core) for i in order]
    for peer in peers[1:] + [neighbour, sibling]:
        pl.semaphore_signal(barrier, inc=1, device_id=peer, device_id_type=MESH)

    values = states_ref[...].astype(jnp.float32)
    scale = lax.rsqrt(jnp.mean(values * values, axis=-1, keepdims=True) + 1e-06)
    normed = (values * scale * gain_ref[...]).astype(jnp.bfloat16)
    ids = ids_ref[...]
    kept = keep_ref[...] > 0
    place = jnp.where(kept, ids * padded + pos_ref[...], -1)
    column = lax.broadcasted_iota(jnp.int32, (tok, slots), 1)
    first = column == place[:, 0:1]
    second = column == place[:, 1:2]
    table = jnp.where(first | second, 1.0, 0.0).astype(jnp.bfloat16)
    mine = jnp.where(core == 0, normed[:, :half], normed[:, half:])
    sent[...] = (
        lax.dot_general(table, mine, (((0,), (0,)), ((), ())), preferred_element_type=jnp.float32)
        .astype(jnp.bfloat16)
        .reshape(experts, padded, half)
    )
    pl.semaphore_wait(barrier, experts + 1)

    pending = []

    def remote(src, dst, send, recv, peer):
        return pltpu.make_async_remote_copy(
            src_ref=src, dst_ref=dst, send_sem=send, recv_sem=recv,
            device_id=peer, device_id_type=MESH,
        )

    def launch(copy):
        copy.start()
        pending.append(copy)

    own = pltpu.make_async_copy(sent.at[group], rows.at[core, side, group], a_recv.at[group])
    own.start()
    for i, peer in zip(order[1:], peers[1:]):
        launch(remote(
            sent.at[flip(group, i)], rows.at[core, side, group],
            a_send.at[flip(group, i)], a_recv.at[group], peer,
        ))

    logits = jnp.dot(normed, router_ref[...], preferred_element_type=jnp.float32)
    expert_column = lax.broadcasted_iota(jnp.int32, (tok, experts), 1)
    score = [
        jax.nn.sigmoid(
            jnp.sum(jnp.where(expert_column == ids[:, n : n + 1], logits, 0.0), axis=1, keepdims=True)
        )
        for n in range(2)
    ]
    total = score[0] + score[1]
    mix = jnp.where(first, score[0] / total, 0.0) + jnp.where(second, score[1] / total, 0.0)
    mix_high = mix.astype(jnp.bfloat16)
    mix_low = (mix - mix_high.astype(jnp.float32)).astype(jnp.bfloat16)

    def share(which, g):
        launch(remote(
            rows.at[core, which, g], rows.at[core, which, g],
            c_send.at[which, g], c_recv.at[which, g], sibling,
        ))

    def take_neighbour(g):
        remote(
            rows.at[core, other_side, g], rows.at[core, other_side, g],
            x_send.at[g], x_recv.at[g], neighbour,
        ).wait_recv()
        share(other_side, g)

    lag = 2
    for n, i in enumerate(order):
        g = flip(group, i)
        if i == 0:
            own.wait()
        else:
            remote(
                sent.at[g], rows.at[core, side, g], a_send.at[g], a_recv.at[g], peers[n]
            ).wait_recv()
        launch(remote(
            rows.at[core, side, g], rows.at[core, side, g], x_send.at[g], x_recv.at[g], neighbour
        ))
        share(side, g)
        if n >= lag:
            take_neighbour(flip(group, order[n - lag]))
    for n in range(max(0, experts - lag), experts):
        take_neighbour(flip(group, order[n]))

    for load in loads:
        load.wait()

    def feed_forward(which):
        for i in order:
            g = flip(group, i)
            remote(
                rows.at[other_core, which, g], rows.at[other_core, which, g],
                c_send.at[which, g], c_recv.at[which, g], sibling,
            ).wait_recv()

        @pl.loop(0, hid.shape[1] // tile)
        def _(n):
            cols = pl.ds(pl.multiple_of(n * tile, tile), tile)
            low = rows[0, which].reshape(slots, half)
            high = rows[1, which].reshape(slots, half)

            def project(w):
                return jnp.dot(
                    low, w[:half, cols], preferred_element_type=jnp.float32
                ) + jnp.dot(high, w[half:, cols], preferred_element_type=jnp.float32)

            hid[:, cols] = (jax.nn.silu(project(wg)) * project(wu)).astype(jnp.bfloat16)

        def down(which_half, n):
            cols = pl.ds(pl.multiple_of(which_half * half + n * tile, tile), tile)
            return jnp.dot(hid[...], wd[:, cols], preferred_element_type=jnp.float32)

        @pl.loop(0, half // tile)
        def _(n):
            cols = pl.ds(pl.multiple_of(n * tile, tile), tile)
            give[which, :, cols] = down(other_core, n).astype(jnp.bfloat16)

        launch(remote(give.at[which], got.at[which], p_send.at[which], p_recv.at[which], sibling))

        @pl.loop(0, half // tile)
        def _(n):
            cols = pl.ds(pl.multiple_of(n * tile, tile), tile)
            acc[which, :, cols] = down(core, n)

    def chip_sum(which, g):
        at = pl.ds(pl.multiple_of(g * padded, padded), padded)
        return acc[which, at, :] + got[which, at, :].astype(jnp.float32)

    def wait_sibling(which):
        remote(
            give.at[which], got.at[which], p_send.at[which], p_recv.at[which], sibling
        ).wait_recv()

    feed_forward(other_side)
    wait_sibling(other_side)
    for i in order:
        g = flip(group, i)
        cross[g] = chip_sum(other_side, g).astype(jnp.bfloat16)
        launch(remote(cross.at[g], crossed.at[g], r_send.at[g], r_recv.at[g], neighbour))

    feed_forward(side)
    wait_sibling(side)
    for n, i in enumerate(order):
        g = flip(group, i)
        remote(cross.at[g], crossed.at[g], r_send.at[g], r_recv.at[g], neighbour).wait_recv()
        whole = (chip_sum(side, g) + crossed[g].astype(jnp.float32)).astype(jnp.bfloat16)
        if i == 0:
            back[g] = whole
        else:
            result[g] = whole
            launch(remote(result.at[g], back.at[group], o_send.at[g], o_recv.at[group], peers[n]))

    for n, i in enumerate(order[1:], 1):
        g = flip(group, i)
        remote(result.at[g], back.at[g], o_send.at[g], o_recv.at[g], peers[n]).wait_recv()
    returned = back[...].reshape(slots, half)
    combined = jnp.dot(mix_high, returned, preferred_element_type=jnp.float32) + jnp.dot(
        mix_low, returned, preferred_element_type=jnp.float32
    )
    residual = jnp.where(core == 0, states_ref[:, :half], states_ref[:, half:]).astype(jnp.float32)
    final[core] = (residual + combined).astype(jnp.bfloat16)
    last = remote(final.at[core], final.at[core], f_send, f_recv, sibling)
    last.start()
    remote(final.at[other_core], final.at[other_core], f_send, f_recv, sibling).wait_recv()
    out_ref[:, :half] = final[0]
    out_ref[:, half:] = final[1]
    last.wait_send()
    for copy in pending:
        copy.wait_send()


def per_device(states, norm_gain, router, w_gate, w_up, w_down, expert_ids, slot_pos, keep_mask):
    tok, width = states.shape
    groups = lax.axis_size("expert")
    experts = router.shape[1]
    assert groups == 2 * experts and lax.axis_size("tensor") == 2
    capacity = max(2, 5 * tok // (2 * experts) + 1)
    padded = -(-capacity // 16) * 16
    half = width // 2
    slots = experts * padded
    units = w_gate.shape[2]
    bf16, f32 = jnp.bfloat16, jnp.float32
    dma = pltpu.SemaphoreType.DMA
    vmem = pl.BlockSpec(memory_space=pltpu.VMEM)
    hbm = pl.BlockSpec(memory_space=pl.ANY)
    return pl.pallas_call(
        functools.partial(kernel, experts, capacity, padded),
        out_shape=jax.ShapeDtypeStruct((tok, width), bf16),
        in_specs=[vmem] * 6 + [hbm] * 3,
        out_specs=vmem,
        scratch_shapes=[
            pltpu.VMEM((width, units), bf16),
            pltpu.VMEM((width, units), bf16),
            pltpu.VMEM((units, width), bf16),
            pltpu.VMEM((experts, padded, half), bf16),
            pltpu.VMEM((2, 2, experts, padded, half), bf16),
            pltpu.VMEM((slots, units), bf16),
            pltpu.VMEM((2, slots, half), bf16),
            pltpu.VMEM((2, slots, half), bf16),
            pltpu.VMEM((2, slots, half), f32),
            pltpu.VMEM((experts, padded, half), bf16),
            pltpu.VMEM((experts, padded, half), bf16),
            pltpu.VMEM((experts, padded, half), bf16),
            pltpu.VMEM((experts, padded, half), bf16),
            pltpu.VMEM((2, tok, half), bf16),
            dma((3,)),
            dma((experts,)), dma((experts,)),
            dma((2, experts)), dma((2, experts)),
            dma((experts,)), dma((experts,)),
            dma((2,)), dma((2,)),
            dma((experts,)), dma((experts,)),
            dma((experts,)), dma((experts,)),
            dma, dma,
        ],
        compiler_params=pltpu.CompilerParams(
            collective_id=0, has_side_effects=True, vmem_limit_bytes=60 * 1024 * 1024
        ),
    )(states, norm_gain.reshape(1, width), router, expert_ids, slot_pos, keep_mask, w_gate, w_up, w_down)


def solution(mesh):
    placed = (
        P("expert", None),
        P(),
        P(),
        P("expert", None, "tensor"),
        P("expert", None, "tensor"),
        P("expert", "tensor", None),
        P("expert", None),
        P("expert", None),
        P("expert", None),
    )
    return jax.shard_map(
        per_device, mesh=mesh, in_specs=placed, out_specs=P("expert", None), check_vma=False
    )
```

time: 164 us -> 66 us (0.40)
  blocking collectives: 65.3 us -> 0 us
  Pallas kernels: 0 us -> 56.7 us
  waiting for transfers between devices: 26.9 us -> 0 us
  matrix products: 17.2 us -> 0 us
  between operations: 13.5 us -> 0.01 us
  local copies, waits for them, and re-layouts: 21.7 us -> 8.92 us
  other arithmetic: 10.7 us -> 0 us
  starting transfers between devices: 6.94 us -> 0 us
    all_to_all x1 -> x0, blocking collectives: 63.2 us -> none  [per_device(): lax.all_to_all(outgoing, 'expert', split_axis=0, concat_axis=0, tiled=True)]
    pallas_call x0 -> x1, Pallas kernels: none -> 56.7 us  [per_device(): pl.pallas_call(functools.partial(kernel, experts, capacity, padded), out_...]
    all_to_all x1 -> x0, waiting for transfers between devices: 19.1 us -> none  [per_device(): lax.all_to_all(summed.astype(jnp.bfloat16), 'expert', split_axis=0, conca...]
    dot_general x5 -> x0, matrix products: 17.2 us -> none  [the longest x1 5.27 us: per_device(): partial_out = jnp.dot(hidden, w_down[0], preferred_element_type=jnp.float32)]
    reduce_scatter x1 -> x0, waiting for transfers between devices: 7.85 us -> none  [per_device(): lax.psum_scatter(partial_out.astype(jnp.bfloat16), 'tensor', scatter_dime...]
    all_to_all x1 -> x0, starting transfers between devices: 6.94 us -> none  [per_device(): lax.all_to_all(summed.astype(jnp.bfloat16), 'expert', split_axis=0, conca...]
    unnamed x11 -> x5, local copies, waits for them, and re-layouts: 1.28 us -> 7.63 us
    reduce_sum x4 -> x0, other arithmetic: 5.75 us -> none  [the longest x1 2.45 us: per_device(): jnp.sum(returned.reshape(all_experts, holders, capacity, out_width), axis=1)]
  transfers between devices with their start and end apart: 2 -> 0, of which waited for: 2 -> 0; matrix products, arithmetic and copies ran while one was open for 5% -> 0% of each run, Pallas kernels for 0% -> 0%
where the time goes in v1:
time: 66 us; the launch traced here: 65.7 us
  Pallas kernels  56.7 us (86%)
  local copies, waits for them, and re-layouts  8.92 us (14%)
    pallas_call x1, Pallas kernels, per_device(): pl.pallas_call(functools.partial(kernel, experts, capacity, padded), out_...  56.7 us
    unnamed x5, local copies, waits for them, and re-layouts  7.63 us

profile of v1, /device:TPU:0, one launch (start us, length us, event | category | flops | bytes accessed | tf_op | source)
XLA Modules:
  0.0 65.7 jit_solution(5238883459745280828)
XLA Ops:
  0.0 1.3 %reshape.3.gain_ref = f32[1,1536]{1,0:T(1,128)} reshape(f32[1536]{0:T(1024)} %param.10) | data formatting | bytes 12288 | tf_op jit(solution)/shard_map/reshape | solution.py:275
  1.3 1.4 %copy.11.ids_ref = s32[128,2]{1,0:T(8,128)} copy(s32[128,2]{0,1:T(2,128)} %param.15) | data formatting | bytes 2048 | tf_op args[6]
  2.7 1.4 %copy.12.pos_ref = s32[128,2]{1,0:T(8,128)} copy(s32[128,2]{0,1:T(2,128)} %param.16) | data formatting | bytes 2048 | tf_op args[7]
  4.1 1.4 %copy.13.keep_ref = s32[128,2]{1,0:T(8,128)} copy(s32[128,2]{0,1:T(2,128)} %param.17) | data formatting | bytes 2048 | tf_op args[8]
  5.5 1.7 %copy.10.router_ref = bf16[1536,8]{1,0:T(8,128)(2,1)} copy(bf16[1536,8]{0,1:T(8,128)(2,1)} %param.11) | data formatting | bytes 49152 | tf_op args[2]
  7.2 56.7 %shard_map.91 = bf16[128,1536]{1,0:T(8,128)(2,1)} custom-call(bf16[128,1536]{1,0:T(8,128)(2,1)} %states_ref.1, f32[1,1536]{1,0:T(1,128)} %reshape.3.gain_ref, bf16[1536,8]{1,0:T(8,128)(2,1)} %copy.10.router_ref, s32[128,2]{1,0:T(8,128)} %copy.11.ids_ref, s32[128,2]{1,0:T(8,128)} %copy.12.pos_ref, s32[128,2]{1,0:T(8,128)} %copy.13.keep_ref, ...), custom_call_target="tpu_custom_call" | custom-call | tf_op jit(solution)/shard_map/pallas_call | solution.py:243
  63.9 1.8 %copy.15 = bf16[128,1536]{1,0:T(8,128)(2,1)} copy(bf16[128,1536]{1,0:T(8,128)(2,1)} %shard_map.91) | data formatting | bytes 786432

commit v2 on v1

--- a/solution.py
+++ b/solution.py
@@ -59,17 +59,17 @@
 
     values = states_ref[...].astype(jnp.float32)
     scale = lax.rsqrt(jnp.mean(values * values, axis=-1, keepdims=True) + 1e-06)
-    normed = (values * scale * gain_ref[...]).astype(jnp.bfloat16)
+    normed = (values * scale * gain_ref[...].reshape(1, width)).astype(jnp.bfloat16)
     ids = ids_ref[...]
     kept = keep_ref[...] > 0
     place = jnp.where(kept, ids * padded + pos_ref[...], -1)
-    column = lax.broadcasted_iota(jnp.int32, (tok, slots), 1)
-    first = column == place[:, 0:1]
-    second = column == place[:, 1:2]
+    slot = lax.broadcasted_iota(jnp.int32, (slots, tok), 0)
+    first = slot == place[0:1, :]
+    second = slot == place[1:2, :]
     table = jnp.where(first | second, 1.0, 0.0).astype(jnp.bfloat16)
     mine = jnp.where(core == 0, normed[:, :half], normed[:, half:])
     sent[...] = (
-        lax.dot_general(table, mine, (((0,), (0,)), ((), ())), preferred_element_type=jnp.float32)
+        jnp.dot(table, mine, preferred_element_type=jnp.float32)
         .astype(jnp.bfloat16)
         .reshape(experts, padded, half)
     )
@@ -95,11 +95,13 @@
             a_send.at[flip(group, i)], a_recv.at[group], peer,
         ))
 
-    logits = jnp.dot(normed, router_ref[...], preferred_element_type=jnp.float32)
-    expert_column = lax.broadcasted_iota(jnp.int32, (tok, experts), 1)
+    logits = lax.dot_general(
+        router_ref[...], normed, (((1,), (1,)), ((), ())), preferred_element_type=jnp.float32
+    )
+    expert_row = lax.broadcasted_iota(jnp.int32, (experts, tok), 0)
     score = [
         jax.nn.sigmoid(
-            jnp.sum(jnp.where(expert_column == ids[:, n : n + 1], logits, 0.0), axis=1, keepdims=True)
+            jnp.sum(jnp.where(expert_row == ids[n : n + 1, :], logits, 0.0), axis=0, keepdims=True)
         )
         for n in range(2)
     ]
@@ -121,10 +123,13 @@
         ).wait_recv()
         share(other_side, g)
 
-    lag = 2
-    for n, i in enumerate(order):
-        g = flip(group, i)
-        if i == 0:
+    lag = 3
+    places = [flip(group, i) for i in order]
+    split = experts // 2
+
+    def step(n):
+        g = places[n]
+        if n == 0:
             own.wait()
         else:
             remote(
@@ -135,26 +140,38 @@
         ))
         share(side, g)
         if n >= lag:
-            take_neighbour(flip(group, order[n - lag]))
-    for n in range(max(0, experts - lag), experts):
-        take_neighbour(flip(group, order[n]))
+            take_neighbour(places[n - lag])
+
+    for n in range(split + lag):
+        step(n)
+    tasks = [functools.partial(step, n) for n in range(split + lag, experts)]
+    tasks += [functools.partial(take_neighbour, places[n]) for n in range(experts - lag, experts)]
 
     for load in loads:
         load.wait()
 
-    def feed_forward(which):
-        for i in order:
-            g = flip(group, i)
+    def feed_forward(part, between):
+        members = [(which, places[part * split + n]) for which in (other_side, side) for n in range(split)]
+        for which, g in members:
             remote(
                 rows.at[other_core, which, g], rows.at[other_core, which, g],
                 c_send.at[which, g], c_recv.at[which, g], sibling,
             ).wait_recv()
-
-        @pl.loop(0, hid.shape[1] // tile)
-        def _(n):
-            cols = pl.ds(pl.multiple_of(n * tile, tile), tile)
-            low = rows[0, which].reshape(slots, half)
-            high = rows[1, which].reshape(slots, half)
+        hooks = list(between)
+        units = hid.shape[1] // tile
+        parts = half // tile
+        spread = units + 2 * parts
+        done = [0]
+
+        def relay():
+            done[0] += 1
+            while len(hooks) > len(between) * (spread - done[0]) // spread:
+                hooks.pop(0)()
+
+        for n in range(units):
+            cols = slice(n * tile, (n + 1) * tile)
+            low = jnp.concatenate([rows[0, which, g] for which, g in members], axis=0)
+            high = jnp.concatenate([rows[1, which, g] for which, g in members], axis=0)
 
             def project(w):
                 return jnp.dot(
@@ -162,57 +179,58 @@
                 ) + jnp.dot(high, w[half:, cols], preferred_element_type=jnp.float32)
 
             hid[:, cols] = (jax.nn.silu(project(wg)) * project(wu)).astype(jnp.bfloat16)
+            relay()
 
         def down(which_half, n):
             cols = pl.ds(pl.multiple_of(which_half * half + n * tile, tile), tile)
             return jnp.dot(hid[...], wd[:, cols], preferred_element_type=jnp.float32)
 
-        @pl.loop(0, half // tile)
-        def _(n):
-            cols = pl.ds(pl.multiple_of(n * tile, tile), tile)
-            give[which, :, cols] = down(other_core, n).astype(jnp.bfloat16)
-
-        launch(remote(give.at[which], got.at[which], p_send.at[which], p_recv.at[which], sibling))
-
-        @pl.loop(0, half // tile)
-        def _(n):
-            cols = pl.ds(pl.multiple_of(n * tile, tile), tile)
-            acc[which, :, cols] = down(core, n)
-
-    def chip_sum(which, g):
-        at = pl.ds(pl.multiple_of(g * padded, padded), padded)
-        return acc[which, at, :] + got[which, at, :].astype(jnp.float32)
-
-    def wait_sibling(which):
-        remote(
-            give.at[which], got.at[which], p_send.at[which], p_recv.at[which], sibling
-        ).wait_recv()
-
-    feed_forward(other_side)
-    wait_sibling(other_side)
-    for i in order:
-        g = flip(group, i)
-        cross[g] = chip_sum(other_side, g).astype(jnp.bfloat16)
-        launch(remote(cross.at[g], crossed.at[g], r_send.at[g], r_recv.at[g], neighbour))
-
-    feed_forward(side)
-    wait_sibling(side)
-    for n, i in enumerate(order):
-        g = flip(group, i)
+        for n in range(parts):
+            cols = slice(n * tile, (n + 1) * tile)
+            give[part, :, cols] = down(other_core, n).astype(jnp.bfloat16)
+            relay()
+        launch(remote(give.at[part], got.at[part], p_send.at[part], p_recv.at[part], sibling))
+        for n in range(parts):
+            cols = slice(n * tile, (n + 1) * tile)
+            acc[part, :, cols] = down(core, n)
+            relay()
+
+    def chip_sum(from_side, n):
+        part, at = n // split, (from_side * split + n % split) * padded
+        at = slice(at, at + padded)
+        return acc[part, at, :] + got[part, at, :].astype(jnp.float32)
+
+    def send_across(part):
+        remote(give.at[part], got.at[part], p_send.at[part], p_recv.at[part], sibling).wait_recv()
+        for n in range(part * split, (part + 1) * split):
+            g = places[n]
+            cross[g] = chip_sum(0, n).astype(jnp.bfloat16)
+            launch(remote(cross.at[g], crossed.at[g], r_send.at[g], r_recv.at[g], neighbour))
+
+    def finish(n):
+        g = places[n]
         remote(cross.at[g], crossed.at[g], r_send.at[g], r_recv.at[g], neighbour).wait_recv()
-        whole = (chip_sum(side, g) + crossed[g].astype(jnp.float32)).astype(jnp.bfloat16)
-        if i == 0:
+        whole = (chip_sum(1, n) + crossed[g].astype(jnp.float32)).astype(jnp.bfloat16)
+        if n == 0:
             back[g] = whole
         else:
             result[g] = whole
             launch(remote(result.at[g], back.at[group], o_send.at[g], o_recv.at[group], peers[n]))
 
+    feed_forward(0, tasks)
+    send_across(0)
+    feed_forward(1, ())
+    send_across(1)
+    for n in range(experts):
+        finish(n)
+
     for n, i in enumerate(order[1:], 1):
         g = flip(group, i)
         remote(result.at[g], back.at[g], o_send.at[g], o_recv.at[g], peers[n]).wait_recv()
     returned = back[...].reshape(slots, half)
-    combined = jnp.dot(mix_high, returned, preferred_element_type=jnp.float32) + jnp.dot(
-        mix_low, returned, preferred_element_type=jnp.float32
+    combined = sum(
+        lax.dot_general(part, returned, (((0,), (0,)), ((), ())), preferred_element_type=jnp.float32)
+        for part in (mix_high, mix_low)
     )
     residual = jnp.where(core == 0, states_ref[:, :half], states_ref[:, half:]).astype(jnp.float32)
     final[core] = (residual + combined).astype(jnp.bfloat16)
@@ -272,7 +290,7 @@
         compiler_params=pltpu.CompilerParams(
             collective_id=0, has_side_effects=True, vmem_limit_bytes=60 * 1024 * 1024
         ),
-    )(states, norm_gain.reshape(1, width), router, expert_ids, slot_pos, keep_mask, w_gate, w_up, w_down)
+    )(states, norm_gain, router.T, expert_ids.T, slot_pos.T, keep_mask.T, w_gate, w_up, w_down)
 
 
 def solution(mesh):

time: 66 us -> 53 us (0.80)
  local copies, waits for them, and re-layouts: 8.92 us -> 1.77 us
  Pallas kernels: 56.7 us -> 51 us
    unnamed x5 -> x1, local copies, waits for them, and re-layouts: 7.63 us -> 1.77 us
    pallas_call x1, Pallas kernels: 56.7 us -> 51 us  [per_device(): pl.pallas_call(functools.partial(kernel, experts, capacity, padded), out_...]
    reshape x1 -> x0, local copies, waits for them, and re-layouts: 1.3 us -> none  [per_device(): norm_gain.reshape(1, width)]
where the time goes in v2:
time: 53 us; the launch traced here: 52.8 us
  Pallas kernels  51 us (96%)
  local copies, waits for them, and re-layouts  1.77 us (3%)
    pallas_call x1, Pallas kernels, per_device(): pl.pallas_call(functools.partial(kernel, experts, capacity, padded), out_...  51 us
    unnamed x1, local copies, waits for them, and re-layouts  1.77 us

profile of v2, /device:TPU:0, one launch (start us, length us, event | category | flops | bytes accessed | tf_op | source)
XLA Modules:
  0.0 52.8 jit_solution(12042026967228117788)
XLA Ops:
  0.0 51.0 %shard_map.91 = bf16[128,1536]{1,0:T(8,128)(2,1)} custom-call(bf16[128,1536]{1,0:T(8,128)(2,1)} %states_ref.1, f32[1536]{0:T(1024)} %gain_ref.1, bf16[8,1536]{1,0:T(8,128)(2,1)} %bitcast.4, s32[2,128]{1,0:T(2,128)} %bitcast.5, s32[2,128]{1,0:T(2,128)} %bitcast.6, s32[2,128]{1,0:T(2,128)} %bitcast.7, bf16[1,1536,1024]{2,1,0:T(8,128)(2,1)} %wg_hbm.1, ...), custom_call_target="tpu_custom_call" | custom-call | tf_op jit(solution)/shard_map/pallas_call | solution.py:261
  51.0 1.8 %copy.11 = bf16[128,1536]{1,0:T(8,128)(2,1)} copy(bf16[128,1536]{1,0:T(8,128)(2,1)} %shard_map.91) | data formatting | bytes 786432
